TPU v7x, 32 devices: a whole 2x2x4 slice. The times are simulated.
32 devices in a mesh: gx: 4 (over x, core), gy: 8 (over z, y).
Axes of the slice: x: 2, y: 2, z: 4, core: 2. Of those that a mesh axis runs over, the one named last changes fastest.
Arguments:
- residual: float32 [2, 524288], P(None, ('gx', 'gy')), may hold values from -15 to 15
- cam_jacobian: float32 [2, 9, 524288], P(None, None, ('gx', 'gy')), may hold values from -0.3 to 0.3
- point_jacobian: float32 [2, 3, 524288], P(None, None, ('gx', 'gy')), may hold values from -1.5 to 1.5
- obs_camera: int32 [524288], P(('gx', 'gy')), may hold values from 0 to 4095
- obs_slot: int32 [524288], P(('gx', 'gy')), may hold values from 0 to 127, as said below
- tile_offset: int32 [1024], P(('gx', 'gy')), may hold values from 0 to 1920, as said below
- damping: float32 [65536], P(('gx', 'gy')), may hold values from 0.3 to 3
- camera_slot: int32 [4096], replicated, may hold values from 0 to 4095, as said below
Outputs:
- reduced: float32 [9, 4096], P(None, ('gx', 'gy'))
- cost: float32 [], replicated
- grad_norm: float32 [], replicated
Inputs may be any that keep to these rules, and one draw needn't show every extreme that they name: `obs_slot`: on each device observations are ordered by point; every observation's point lies in its tile's window of 128 points starting at tile_offset. `tile_offset`: windows lie within the device's 2048 points and do not fall from tile to tile. `camera_slot`: each position of the owners' layout is taken by exactly one camera.
All inputs are finite; a program needn't handle non-finite values.
Results may differ from a plain program's by a relative error of at most 0.000096.
Values sent between devices are 32-bit elements; how exact they have to be, the bound alone decides.
A program may use at most 64 MiB of HBM per device.

v0:
```python
import jax
import jax.numpy as jnp
from jax import lax
from jax.sharding import PartitionSpec as P


def block_solve(entries, rhs):
    comp_aa = entries[0]
    comp_ab = entries[1]
    comp_ac = entries[2]
    comp_bb = entries[3]
    comp_bc = entries[4]
    comp_cc = entries[5]
    cof_aa = comp_bb * comp_cc - comp_bc * comp_bc
    cof_ab = comp_ac * comp_bc - comp_ab * comp_cc
    cof_ac = comp_ab * comp_bc - comp_ac * comp_bb
    cof_bb = comp_aa * comp_cc - comp_ac * comp_ac
    cof_bc = comp_ab * comp_ac - comp_aa * comp_bc
    cof_cc = comp_aa * comp_bb - comp_ab * comp_ab
    determ = comp_aa * cof_aa + comp_ab * cof_ab + comp_ac * cof_ac
    first = (cof_aa * rhs[0] + cof_ab * rhs[1] + cof_ac * rhs[2]) / determ
    second = (cof_ab * rhs[0] + cof_bb * rhs[1] + cof_bc * rhs[2]) / determ
    third = (cof_ac * rhs[0] + cof_bc * rhs[1] + cof_cc * rhs[2]) / determ
    return jnp.stack([first, second, third])


def point_features(residual, point_jacobian):
    grad_obs = jnp.sum(point_jacobian * residual[:, None, :], axis=0)
    pairs = [(0, 0), (0, 1), (0, 2), (1, 1), (1, 2), (2, 2)]
    products = [
        jnp.sum(point_jacobian[:, left] * point_jacobian[:, right], axis=0) for left, right in pairs
    ]
    return jnp.concatenate([grad_obs, jnp.stack(products)], axis=0)


def block_length(n_obs):
    return min(n_obs, max(512, n_obs // 16))


def onehot_sums(values, index, count):
    rows, n_obs = values.shape
    length = block_length(n_obs)
    blocks = n_obs // length
    value_blocks = jnp.moveaxis(values.reshape(rows, blocks, length), 1, 0)
    index_blocks = index.reshape(blocks, length)
    columns = jnp.arange(count, dtype=jnp.int32)

    def add_block(total, pair):
        block_values, block_index = pair
        onehot = (block_index[:, None] == columns[None, :]).astype(jnp.float32)
        return (total + jnp.dot(block_values, onehot, precision=lax.Precision.HIGHEST), None)

    start = jnp.zeros((rows, count), jnp.float32)
    total, _ = lax.scan(add_block, start, (value_blocks, index_blocks))
    return total


def onehot_take(table, index):
    rows, count = table.shape
    n_obs = index.shape[0]
    length = block_length(n_obs)
    blocks = n_obs // length
    index_blocks = index.reshape(blocks, length)
    columns = jnp.arange(count, dtype=jnp.int32)

    def take_block(block_index):
        onehot = (columns[:, None] == block_index[None, :]).astype(jnp.float32)
        return jnp.dot(table, onehot, precision=lax.Precision.HIGHEST)

    taken = lax.map(take_block, index_blocks)
    return jnp.moveaxis(taken, 0, 1).reshape(rows, n_obs)


def on_device(
    residual, cam_jacobian, point_jacobian, obs_camera, obs_slot, tile_offset, damping, camera_slot
):
    n_obs = residual.shape[1]
    n_tiles = tile_offset.shape[0]
    tile_len = n_obs // n_tiles
    point_count = damping.shape[0]
    camera_count = camera_slot.shape[0]
    devices = lax.axis_size(("gx", "gy"))
    cam_slots = camera_slot[obs_camera]
    grad_obs = jnp.sum(cam_jacobian * residual[:, None, :], axis=0)
    cost_part = jnp.sum(residual * residual)
    features = point_features(residual, point_jacobian)
    slot_tiles = obs_slot.reshape(n_tiles, tile_len)
    point_index = (tile_offset[:, None] + slot_tiles).reshape(-1)
    point_sums = onehot_sums(features, point_index, point_count)
    point_grad = point_sums[:3]
    diag_mask = jnp.array([1.0, 0.0, 0.0, 1.0, 0.0, 1.0], jnp.float32)[:, None]
    entries = point_sums[3:] + diag_mask * damping[None, :]
    step_point = block_solve(entries, point_grad)
    step_obs = onehot_take(step_point, point_index)
    moved = jnp.sum(point_jacobian * step_obs[None, :, :], axis=1)
    coupling_obs = jnp.sum(cam_jacobian * moved[:, None, :], axis=0)
    point_square = jnp.sum(point_grad * point_grad)
    cost_total, point_total = lax.psum((cost_part, point_square), ("gx", "gy"))
    both_obs = jnp.concatenate([grad_obs, coupling_obs], axis=0)
    both_buffer = onehot_sums(both_obs, cam_slots, camera_count)
    both_share = lax.psum_scatter(both_buffer, ("gx", "gy"), scatter_dimension=1, tiled=True)
    grad_share = both_share[:9]
    coupling_share = both_share[9:]
    reduced = coupling_share - grad_share
    camera_square = jnp.sum(grad_share * grad_share)
    camera_sum = lax.psum(camera_square, ("gx", "gy"))
    cost = cost_total / (2.0 * n_obs * devices)
    grad_norm = jnp.sqrt(
        (camera_sum + point_total) / (9.0 * camera_count + 3.0 * point_count * devices) + 1e-06
    )
    return (reduced, cost, grad_norm)


def solution(mesh):
    return jax.shard_map(
        on_device,
        mesh=mesh,
        in_specs=(
            P(None, ("gx", "gy")),
            P(None, None, ("gx", "gy")),
            P(None, None, ("gx", "gy")),
            P(("gx", "gy")),
            P(("gx", "gy")),
            P(("gx", "gy")),
            P(("gx", "gy")),
            P(),
        ),
        out_specs=(P(None, ("gx", "gy")), P(), P()),
        check_vma=False,
    )
```

profile of v0, /device:TPU:0, one launch (start us, length us, event | category | flops | bytes accessed | tf_op | source)
XLA Modules:
  0.0 475.0 jit_solution(6179759040438174137)
XLA Ops:
  12.0 44.6 %while.34 = (s32[]{:T(128)}, f32[9,2048]{1,0:T(8,128)S(1)}, f32[16,9,1024]{2,1,0:T(8,128)S(1)}, s32[16,1024]{1,0:T(8,128)S(1)}, s32[]{:T(128)}, /*index=5*/s32[]{:T(128)}) while((s32[]{:T(128)}, f32[9,2048]{1,0:T(8,128)S(1)}, f32[16,9,1024]{2,1,0:T(8,128)S(1)}, s32[16,1024]{1,0:T(8,128)S(1)}, s32[]{:T(128)}, ...), condition=%wide.region_9.10_spmd.clone, body=%wide.region_8.0_spmd.clone.sunk | while | flops 228626432 | bytes 282711 | solution.py:54
  12.1 2.8 fusion.29
  14.9 2.8 fusion.29
  17.6 2.8 fusion.29
  20.4 2.8 fusion.29
  23.2 2.8 fusion.29
  26.0 2.8 fusion.29
  31.6 2.8 fusion.29
  40.0 2.8 fusion.29
  48.3 2.8 fusion.29
  57.0 42.6 %while.33 = (s32[]{:T(128)}, f32[16,3,1024]{2,1,0:T(4,128)S(1)}, s32[16,1024]{1,0:T(8,128)S(1)}, f32[3,2048]{1,0:T(4,128)S(1)}, s32[]{:T(128)}) while((s32[]{:T(128)}, f32[16,3,1024]{2,1,0:T(4,128)S(1)}, s32[16,1024]{1,0:T(8,128)S(1)}, f32[3,2048]{1,0:T(4,128)S(1)}, s32[]{:T(128)}) %tuple.83), condition=%wide.region_11.12_spmd.clone, body=%wide.region_10.11_spmd.clone.sunk | while | flops 77594624 | bytes 61509 | solution.py:70
  99.9 3.0 multiply_reduce_fusion.1
  104.8 90.5 %gather_fusion = s32[16384]{0:T(1024)S(1)} fusion(s32[4096]{0:T(1024)S(1)} %copy-done, s32[16384]{0:T(1024)S(1)} %fusion.19), kind=kCustom, calls=%fused_computation | custom fusion | bytes 196608 | tf_op jit(solution)/shard_map/gather | solution.py:83
  195.4 89.4 %while.35 = (s32[]{:T(128)}, f32[18,4096]{1,0:T(8,128)S(1)}, f32[16,18,1024]{2,0,1:T(8,128)S(1)}, s32[16,1024]{1,0:T(8,128)S(1)}, s32[]{:T(128)}, /*index=5*/s32[]{:T(128)}) while((s32[]{:T(128)}, f32[18,4096]{1,0:T(8,128)S(1)}, f32[16,18,1024]{2,0,1:T(8,128)S(1)}, s32[16,1024]{1,0:T(8,128)S(1)}, s32[]{:T(128)}, ...), condition=%wide.region_15.16_spmd.clone, body=%wide.region_14.15_spmd.clone.sunk | while | flops 910311424 | bytes 823383 | solution.py:54
  195.6 5.5 %fusion.30 = f32[18,4096]{1,0:T(8,128)S(1)} fusion(s32[1024]{0:T(1024)S(1)} %bitcast.61, f32[18,4096]{1,0:T(8,128)S(1)} %get-tuple-element.292, pred[]{:T(512)S(6)} %compare.7, f32[1,18,1024]{2,0,1:T(1,128)S(1)} %constant_dynamic-slice_fusion.11), kind=kOutput, calls=%fused_computation.21.clone.1 | convolution fusion | flops 910311424 | bytes 667649 | tf_op jit(solution)/shard_map/while/body/eval_jaxpr/dot_general | solution.py:51
  201.2 5.5 %fusion.30 = f32[18,4096]{1,0:T(8,128)S(1)} fusion(s32[1024]{0:T(1024)S(1)} %bitcast.61, f32[18,4096]{1,0:T(8,128)S(1)} %get-tuple-element.292, pred[]{:T(512)S(6)} %compare.7, f32[1,18,1024]{2,0,1:T(1,128)S(1)} %constant_dynamic-slice_fusion.11), kind=kOutput, calls=%fused_computation.21.clone.1 | convolution fusion | flops 910311424 | bytes 667649 | tf_op jit(solution)/shard_map/while/body/eval_jaxpr/dot_general | solution.py:51
  206.8 5.5 %fusion.30 = f32[18,4096]{1,0:T(8,128)S(1)} fusion(s32[1024]{0:T(1024)S(1)} %bitcast.61, f32[18,4096]{1,0:T(8,128)S(1)} %get-tuple-element.292, pred[]{:T(512)S(6)} %compare.7, f32[1,18,1024]{2,0,1:T(1,128)S(1)} %constant_dynamic-slice_fusion.11), kind=kOutput, calls=%fused_computation.21.clone.1 | convolution fusion | flops 910311424 | bytes 667649 | tf_op jit(solution)/shard_map/while/body/eval_jaxpr/dot_general | solution.py:51
  212.4 5.5 %fusion.30 = f32[18,4096]{1,0:T(8,128)S(1)} fusion(s32[1024]{0:T(1024)S(1)} %bitcast.61, f32[18,4096]{1,0:T(8,128)S(1)} %get-tuple-element.292, pred[]{:T(512)S(6)} %compare.7, f32[1,18,1024]{2,0,1:T(1,128)S(1)} %constant_dynamic-slice_fusion.11), kind=kOutput, calls=%fused_computation.21.clone.1 | convolution fusion | flops 910311424 | bytes 667649 | tf_op jit(solution)/shard_map/while/body/eval_jaxpr/dot_general | solution.py:51
  217.9 5.5 %fusion.30 = f32[18,4096]{1,0:T(8,128)S(1)} fusion(s32[1024]{0:T(1024)S(1)} %bitcast.61, f32[18,4096]{1,0:T(8,128)S(1)} %get-tuple-element.292, pred[]{:T(512)S(6)} %compare.7, f32[1,18,1024]{2,0,1:T(1,128)S(1)} %constant_dynamic-slice_fusion.11), kind=kOutput, calls=%fused_computation.21.clone.1 | convolution fusion | flops 910311424 | bytes 667649 | tf_op jit(solution)/shard_map/while/body/eval_jaxpr/dot_general | solution.py:51
  223.5 5.5 %fusion.30 = f32[18,4096]{1,0:T(8,128)S(1)} fusion(s32[1024]{0:T(1024)S(1)} %bitcast.61, f32[18,4096]{1,0:T(8,128)S(1)} %get-tuple-element.292, pred[]{:T(512)S(6)} %compare.7, f32[1,18,1024]{2,0,1:T(1,128)S(1)} %constant_dynamic-slice_fusion.11), kind=kOutput, calls=%fused_computation.21.clone.1 | convolution fusion | flops 910311424 | bytes 667649 | tf_op jit(solution)/shard_map/while/body/eval_jaxpr/dot_general | solution.py:51
  229.1 5.5 %fusion.30 = f32[18,4096]{1,0:T(8,128)S(1)} fusion(s32[1024]{0:T(1024)S(1)} %bitcast.61, f32[18,4096]{1,0:T(8,128)S(1)} %get-tuple-element.292, pred[]{:T(512)S(6)} %compare.7, f32[1,18,1024]{2,0,1:T(1,128)S(1)} %constant_dynamic-slice_fusion.11), kind=kOutput, calls=%fused_computation.21.clone.1 | convolution fusion | flops 910311424 | bytes 667649 | tf_op jit(solution)/shard_map/while/body/eval_jaxpr/dot_general | solution.py:51
  234.7 5.5 %fusion.30 = f32[18,4096]{1,0:T(8,128)S(1)} fusion(s32[1024]{0:T(1024)S(1)} %bitcast.61, f32[18,4096]{1,0:T(8,128)S(1)} %get-tuple-element.292, pred[]{:T(512)S(6)} %compare.7, f32[1,18,1024]{2,0,1:T(1,128)S(1)} %constant_dynamic-slice_fusion.11), kind=kOutput, calls=%fused_computation.21.clone.1 | convolution fusion | flops 910311424 | bytes 667649 | tf_op jit(solution)/shard_map/while/body/eval_jaxpr/dot_general | solution.py:51
  240.2 5.5 %fusion.30 = f32[18,4096]{1,0:T(8,128)S(1)} fusion(s32[1024]{0:T(1024)S(1)} %bitcast.61, f32[18,4096]{1,0:T(8,128)S(1)} %get-tuple-element.292, pred[]{:T(512)S(6)} %compare.7, f32[1,18,1024]{2,0,1:T(1,128)S(1)} %constant_dynamic-slice_fusion.11), kind=kOutput, calls=%fused_computation.21.clone.1 | convolution fusion | flops 910311424 | bytes 667649 | tf_op jit(solution)/shard_map/while/body/eval_jaxpr/dot_general | solution.py:51
  245.8 5.5 %fusion.30 = f32[18,4096]{1,0:T(8,128)S(1)} fusion(s32[1024]{0:T(1024)S(1)} %bitcast.61, f32[18,4096]{1,0:T(8,128)S(1)} %get-tuple-element.292, pred[]{:T(512)S(6)} %compare.7, f32[1,18,1024]{2,0,1:T(1,128)S(1)} %constant_dynamic-slice_fusion.11), kind=kOutput, calls=%fused_computation.21.clone.1 | convolution fusion | flops 910311424 | bytes 667649 | tf_op jit(solution)/shard_map/while/body/eval_jaxpr/dot_general | solution.py:51
  251.4 5.5 %fusion.30 = f32[18,4096]{1,0:T(8,128)S(1)} fusion(s32[1024]{0:T(1024)S(1)} %bitcast.61, f32[18,4096]{1,0:T(8,128)S(1)} %get-tuple-element.292, pred[]{:T(512)S(6)} %compare.7, f32[1,18,1024]{2,0,1:T(1,128)S(1)} %constant_dynamic-slice_fusion.11), kind=kOutput, calls=%fused_computation.21.clone.1 | convolution fusion | flops 910311424 | bytes 667649 | tf_op jit(solution)/shard_map/while/body/eval_jaxpr/dot_general | solution.py:51
  257.0 5.5 %fusion.30 = f32[18,4096]{1,0:T(8,128)S(1)} fusion(s32[1024]{0:T(1024)S(1)} %bitcast.61, f32[18,4096]{1,0:T(8,128)S(1)} %get-tuple-element.292, pred[]{:T(512)S(6)} %compare.7, f32[1,18,1024]{2,0,1:T(1,128)S(1)} %constant_dynamic-slice_fusion.11), kind=kOutput, calls=%fused_computation.21.clone.1 | convolution fusion | flops 910311424 | bytes 667649 | tf_op jit(solution)/shard_map/while/body/eval_jaxpr/dot_general | solution.py:51
  262.5 5.5 %fusion.30 = f32[18,4096]{1,0:T(8,128)S(1)} fusion(s32[1024]{0:T(1024)S(1)} %bitcast.61, f32[18,4096]{1,0:T(8,128)S(1)} %get-tuple-element.292, pred[]{:T(512)S(6)} %compare.7, f32[1,18,1024]{2,0,1:T(1,128)S(1)} %constant_dynamic-slice_fusion.11), kind=kOutput, calls=%fused_computation.21.clone.1 | convolution fusion | flops 910311424 | bytes 667649 | tf_op jit(solution)/shard_map/while/body/eval_jaxpr/dot_general | solution.py:51
  268.1 5.5 %fusion.30 = f32[18,4096]{1,0:T(8,128)S(1)} fusion(s32[1024]{0:T(1024)S(1)} %bitcast.61, f32[18,4096]{1,0:T(8,128)S(1)} %get-tuple-element.292, pred[]{:T(512)S(6)} %compare.7, f32[1,18,1024]{2,0,1:T(1,128)S(1)} %constant_dynamic-slice_fusion.11), kind=kOutput, calls=%fused_computation.21.clone.1 | convolution fusion | flops 910311424 | bytes 667649 | tf_op jit(solution)/shard_map/while/body/eval_jaxpr/dot_general | solution.py:51
  273.7 5.5 %fusion.30 = f32[18,4096]{1,0:T(8,128)S(1)} fusion(s32[1024]{0:T(1024)S(1)} %bitcast.61, f32[18,4096]{1,0:T(8,128)S(1)} %get-tuple-element.292, pred[]{:T(512)S(6)} %compare.7, f32[1,18,1024]{2,0,1:T(1,128)S(1)} %constant_dynamic-slice_fusion.11), kind=kOutput, calls=%fused_computation.21.clone.1 | convolution fusion | flops 910311424 | bytes 667649 | tf_op jit(solution)/shard_map/while/body/eval_jaxpr/dot_general | solution.py:51
  279.3 5.5 %fusion.30 = f32[18,4096]{1,0:T(8,128)S(1)} fusion(s32[1024]{0:T(1024)S(1)} %bitcast.61, f32[18,4096]{1,0:T(8,128)S(1)} %get-tuple-element.292, pred[]{:T(512)S(6)} %compare.7, f32[1,18,1024]{2,0,1:T(1,128)S(1)} %constant_dynamic-slice_fusion.11), kind=kOutput, calls=%fused_computation.21.clone.1 | convolution fusion | flops 910311424 | bytes 667649 | tf_op jit(solution)/shard_map/while/body/eval_jaxpr/dot_general | solution.py:51
  286.9 137.3 %reduce-scatter.2.cloned.1.call-done = f32[18,128]{1,0:T(8,128)} async-done(((f32[18,4096]{1,0:T(8,128)}), f32[18,128]{1,0:T(8,128)}) %reduce-scatter.2.cloned.1.call-update) | async-done | bytes 9232 | tf_op jit(solution)/shard_map/reduce_scatter | solution.py:101
  427.4 37.1 %all-reduce = (f32[]{:T(128)}, f32[]{:T(128)}) all-reduce(f32[]{:T(128)} %multiply_reduce_fusion.4, f32[]{:T(128)S(6)} %add.102), channel_id=1, replica_groups=mesh['gx'=4,'gy'=8] {'gx','gy'}, use_global_device_ids=true, to_apply=%region_18.19 | all-reduce | flops 2 | bytes 16 | tf_op jit(solution)/shard_map/psum | solution.py:98
  (133 shorter events, 74.4 us)
Async XLA Ops:
  7.2 97.6 %copy-start = (s32[4096]{0:T(1024)S(1)}, s32[4096]{0:T(1024)}, u32[]{:S(2)}) copy-start(s32[4096]{0:T(1024)} %param.22) | copy-start | bytes 49156
  7.2 3.8 copy-start.9
  7.2 4.0 copy-start.5
  7.2 417.0 %reduce-scatter.2.cloned.1.call-start = ((), (), s32[]{:S(2)}) async-start(), calls=%async_computation.1 | async-start | bytes 405504 | tf_op jit(solution)/shard_map/reduce_scatter | solution.py:101
  12.0 44.7 %copy-start.7 = (f32[2048]{0:T(1024)S(1)}, f32[2048]{0:T(1024)}, u32[]{:S(2)}) copy-start(f32[2048]{0:T(1024)} %param.21) | copy-start | bytes 24580
  12.0 44.7 %copy-start.8 = (f32[6]{0:T(128)S(1)}, f32[6]{0:T(128)}, u32[]{:S(2)}) copy-start(f32[6]{0:T(128)} %constant.45.clone) | copy-start | bytes 76
  57.0 42.6 %copy-start.1 = (f32[2,3,16384]{2,0,1:T(2,128)S(1)}, f32[2,3,16384]{2,0,1:T(2,128)}, u32[]{:S(2)}) copy-start(f32[2,3,16384]{2,0,1:T(2,128)} %param.17) | copy-start | bytes 1179652
  57.0 42.9 %copy-start.2 = (f32[2,16384]{1,0:T(2,128)S(1)}, f32[2,16384]{1,0:T(2,128)}, u32[]{:S(2)}) copy-start(f32[2,16384]{1,0:T(2,128)} %param.15) | copy-start | bytes 393220
  57.0 42.8 %copy-start.3 = (f32[2,9,16384]{2,0,1:T(2,128)S(1)}, f32[2,9,16384]{2,0,1:T(2,128)}, u32[]{:S(2)}) copy-start(f32[2,9,16384]{2,0,1:T(2,128)} %param.16) | copy-start | bytes 3538948
  103.9 0.8 copy-start.6
  284.7 0.7 copy-start.4
Sparse Core Ops, SparseCore 0:
  285.6 138.5 reduce-scatter.1
where the time goes:
time: 476 us; the launch traced here: 475 us
  matrix products  174 us (37%)
  waiting for transfers between devices  137 us (29%)
  local copies, waits for them, and re-layouts  95.6 us (20%)
  blocking collectives  37.1 us (8%)
  between operations  19.2 us (4%)
  other arithmetic  10.7 us (2%)
    reduce_scatter x1, waiting for transfers between devices, on_device(): lax.psum_scatter(both_buffer, ('gx', 'gy'), scatter_dimension=1, tiled=True)  137 us
    dot_general x32, matrix products, add_block(): jnp.dot(block_values, onehot, precision=lax.Precision.HIGHEST)  132 us
    gather x1, local copies, waits for them, and re-layouts, on_device(): cam_slots = camera_slot[obs_camera]  90.5 us
    dot_general x16, matrix products, take_block(): return jnp.dot(table, onehot, precision=lax.Precision.HIGHEST)  42.2 us
    psum x1, blocking collectives, on_device(): cost_total, point_total = lax.psum((cost_part, point_square), ('gx', 'gy'))  37.1 us
  transfers between devices with their start and end apart: 1, of which 1 were waited for; matrix products, arithmetic and copies ran while one was open for 0% of the time, Pallas kernels for 0%

commit v1 on v0

v1 whole, which is shorter than its diff:
```python
import functools

import jax
import jax.numpy as jnp
from jax import lax
from jax.experimental import pallas as pl
from jax.experimental.pallas import tpu as pltpu
from jax.sharding import PartitionSpec as P

AXES = ("gx", "gy")
MESH = pl.DeviceIdType.MESH
F32 = jnp.float32
BF16 = jnp.bfloat16
LANES = 128
GROUP = 8
LOW_BITS = 8
LOW = 1 << LOW_BITS
PARAMS = 9
FEATURES = 16


def nt_dot(left, right):
    return lax.dot_general(left, right, (((1,), (1,)), ((), ())), preferred_element_type=F32)


def split_pieces(value, pieces):
    out = []
    rest = value
    for _ in range(pieces - 1):
        head = rest.astype(BF16)
        out.append(head)
        rest = rest - head.astype(F32)
    out.append(rest.astype(BF16))
    return out


def lane_take(row, index):
    table = jnp.broadcast_to(row, index.shape)
    return jnp.take_along_axis(table, index, axis=1)


def block_solve(entries, rhs):
    comp_aa, comp_ab, comp_ac, comp_bb, comp_bc, comp_cc = entries
    cof_aa = comp_bb * comp_cc - comp_bc * comp_bc
    cof_ab = comp_ac * comp_bc - comp_ab * comp_cc
    cof_ac = comp_ab * comp_bc - comp_ac * comp_bb
    cof_bb = comp_aa * comp_cc - comp_ac * comp_ac
    cof_bc = comp_ab * comp_ac - comp_aa * comp_bc
    cof_cc = comp_aa * comp_bb - comp_ab * comp_ab
    determ = comp_aa * cof_aa + comp_ab * cof_ab + comp_ac * cof_ac
    first = (cof_aa * rhs[0] + cof_ab * rhs[1] + cof_ac * rhs[2]) / determ
    second = (cof_ab * rhs[0] + cof_bb * rhs[1] + cof_bc * rhs[2]) / determ
    third = (cof_ac * rhs[0] + cof_bc * rhs[1] + cof_cc * rhs[2]) / determ
    return first, second, third


def point_kernel(
    toff_ref, res_ref, pj_ref, cam_ref, slot_ref, damp_ref, cslot_ref,
    w_ref, pos_ref, scal_ref, feat, sums, steps,
):
    rows = cam_ref.shape[0]
    tiles = toff_ref.shape[0]
    tile_rows = rows // tiles
    blocks = damp_ref.shape[0]
    table_rows = cslot_ref.shape[0]
    groups = rows // GROUP
    per_group = max(1, GROUP // tile_rows)

    sums[...] = jnp.zeros_like(sums)
    feat[...] = jnp.zeros_like(feat)

    def pair(ref, group, lead=()):
        return [
            ref[(*lead, pl.ds(group * (2 * GROUP) + part, GROUP, stride=2), slice(None))]
            for part in range(2)
        ]

    def group_step(group, cost):
        at = pl.ds(pl.multiple_of(group * GROUP, GROUP), GROUP)
        camera = cam_ref[at, :]
        high = camera >> 7
        low = camera & (LANES - 1)
        position = jnp.zeros_like(camera)
        for t in range(table_rows):
            position = jnp.where(high == t, lane_take(cslot_ref[t : t + 1, :], low), position)
        pos_ref[at, :] = position
        res = pair(res_ref, group)
        jac = [pair(pj_ref, group, (k,)) for k in range(3)]
        values = [jac[k][0] * res[0] + jac[k][1] * res[1] for k in range(3)]
        for k, l in ((0, 0), (0, 1), (0, 2), (1, 1), (1, 2), (2, 2)):
            values.append(jac[k][0] * jac[l][0] + jac[k][1] * jac[l][1])
        for f, value in enumerate(values):
            feat[pl.ds(group * (GROUP * FEATURES) + f, GROUP, stride=FEATURES), :] = value
        return cost + (res[0] * res[0] + res[1] * res[1])

    cost = lax.fori_loop(0, groups, group_step, jnp.zeros((GROUP, LANES), F32), unroll=2)

    points = lax.broadcasted_iota(jnp.int32, (LANES, LANES), 0)
    lane = lax.broadcasted_iota(jnp.int32, (FEATURES, LANES), 1)
    batch = 4 if tiles % 4 == 0 else 1

    def tile_batch(step, carry):
        totals = []
        for b in range(batch):
            tile = step * batch + b
            left, right = [], []
            for r in range(tile_rows):
                row = tile * tile_rows + r
                start = pl.multiple_of(row * FEATURES, FEATURES)
                pieces = split_pieces(feat[pl.ds(start, FEATURES), :], 3)
                left.append(jnp.concatenate(pieces, axis=0))
                slot = slot_ref[pl.ds(row, 1), :]
                right.append(jnp.where(points == slot, 1.0, 0.0).astype(BF16))
            out = nt_dot(jnp.concatenate(left, axis=1), jnp.concatenate(right, axis=1))
            totals.append(out[:FEATURES] + out[FEATURES : 2 * FEATURES] + out[2 * FEATURES :])
        for b in range(batch):
            offset = toff_ref[step * batch + b]
            block = offset >> 7
            shift = offset & (LANES - 1)
            rolled = pltpu.roll(totals[b], shift, 1)
            sums[block] += jnp.where(lane >= shift, rolled, 0.0)
            sums[block + 1] += jnp.where(lane < shift, rolled, 0.0)
        return carry

    lax.fori_loop(0, tiles // batch, tile_batch, 0)

    damp = damp_ref[...]
    columns = [sums[pl.ds(0, blocks), f, :] for f in range(9)]
    grad = columns[:3]
    entries = [
        col + damp if i in (0, 3, 5) else col for i, col in enumerate(columns[3:])
    ]
    step_point = block_solve(entries, grad)
    for k in range(3):
        steps[k, pl.ds(0, blocks), :] = step_point[k]
        steps[k, pl.ds(blocks, 1), :] = jnp.zeros((1, LANES), F32)
    square = grad[0] * grad[0] + grad[1] * grad[1] + grad[2] * grad[2]
    scal_ref[0:1, :] = jnp.sum(cost, axis=0, keepdims=True)
    scal_ref[1:2, :] = jnp.sum(square, axis=0, keepdims=True)

    sub = lax.broadcasted_iota(jnp.int32, (GROUP, LANES), 0)

    def take_step(group, carry):
        at = pl.ds(pl.multiple_of(group * GROUP, GROUP), GROUP)
        first = (group * GROUP) // tile_rows
        offsets = [toff_ref[first + t] for t in range(per_group)]
        shift = jnp.zeros((GROUP, LANES), jnp.int32) + (offsets[0] & (LANES - 1))
        for t in range(1, per_group):
            shift = jnp.where(sub >= t * tile_rows, offsets[t] & (LANES - 1), shift)
        index = slot_ref[at, :] + shift
        low = index & (LANES - 1)
        inside = index < LANES
        res = pair(res_ref, group)
        moved = [-res[0], -res[1]]
        for k in range(3):
            here = jnp.broadcast_to(steps[k, pl.ds(offsets[0] >> 7, 1), :], (GROUP, LANES))
            after = jnp.broadcast_to(steps[k, pl.ds((offsets[0] >> 7) + 1, 1), :], (GROUP, LANES))
            for t in range(1, per_group):
                later = sub >= t * tile_rows
                here = jnp.where(later, steps[k, pl.ds(offsets[t] >> 7, 1), :], here)
                after = jnp.where(later, steps[k, pl.ds((offsets[t] >> 7) + 1, 1), :], after)
            taken = jnp.where(
                inside,
                jnp.take_along_axis(here, low, axis=1),
                jnp.take_along_axis(after, low, axis=1),
            )
            jac = pair(pj_ref, group, (k,))
            moved = [moved[a] + jac[a] * taken for a in range(2)]
        w_ref[0, at, :] = moved[0]
        w_ref[1, at, :] = moved[1]
        return carry

    lax.fori_loop(0, groups, take_step, 0, unroll=2)


def camera_kernel(
    gx_size, gy_size, cost_scale, norm_scale,
    cj_ref, res_ref, w_ref, pos_ref, scal_ref,
    red_ref, cost_ref, norm_ref,
    acc, left, right, rowbuf, part, pair_in, chip_sum, recv, tot_send, tot_recv,
    pair_sems, chip_send, chip_recv, tot_ssem, tot_rsem,
):
    devices = gx_size * gy_size
    chips = devices // 2
    gx = lax.axis_index("gx")
    gy = lax.axis_index("gy")
    me = gx * gy_size + gy
    core = lax.rem(gx, 2)
    chip = (gx // 2) * gy_size + gy

    barrier = pltpu.get_barrier_semaphore()

    def greet(i, carry):
        peer = lax.rem(me + i, devices)
        pl.semaphore_signal(
            barrier, inc=1, device_id=(peer // gy_size, lax.rem(peer, gy_size)), device_id_type=MESH
        )
        return carry

    lax.fori_loop(1, devices, greet, 0)

    rows = pos_ref.shape[0]
    highs = devices * LANES // LOW
    lows = lax.broadcasted_iota(jnp.int32, (LOW, LANES), 0)
    tops = lax.broadcasted_iota(jnp.int32, (highs, LANES), 0)
    acc[...] = jnp.zeros_like(acc)

    def build(group, buf):
        at = pl.ds(pl.multiple_of(group * GROUP, GROUP), GROUP)
        even = pl.ds(group * (2 * GROUP), GROUP, stride=2)
        odd = pl.ds(group * (2 * GROUP) + 1, GROUP, stride=2)
        res0, res1 = res_ref[even, :], res_ref[odd, :]
        w0, w1 = w_ref[0, at, :], w_ref[1, at, :]
        for m in range(PARAMS):
            jac0, jac1 = cj_ref[m, even, :], cj_ref[m, odd, :]
            for j, value in ((m, jac0 * res0 + jac1 * res1), (m + PARAMS, jac0 * w0 + jac1 * w1)):
                head = value.astype(BF16).astype(F32)
                rowbuf[buf, j] = head
                rowbuf[buf, 2 * PARAMS + j] = value - head
        for r in range(GROUP):
            position = pos_ref[pl.ds(group * GROUP + r, 1), :]
            cols = slice(r * LANES, (r + 1) * LANES)
            right[buf, :, cols] = jnp.where(lows == (position & (LOW - 1)), 1.0, 0.0).astype(BF16)
            top = jnp.where(tops == (position >> LOW_BITS), 1.0, 0.0).astype(BF16)
            for j in range(4 * PARAMS):
                row = jnp.broadcast_to(rowbuf[buf, j, r : r + 1, :], (highs, LANES)).astype(BF16)
                left[buf, j * highs : (j + 1) * highs, cols] = row * top

    def two_groups(step, carry):
        for buf in range(2):
            build(step * 2 + buf, buf)
            acc[...] += nt_dot(left[buf], right[buf])
        return carry

    lax.fori_loop(0, rows // (2 * GROUP), two_groups, 0)

    for dest in range(devices):
        dgx, dgy = dest // gy_size, dest % gy_size
        half = slice((dest % 2) * LANES, (dest % 2 + 1) * LANES)
        top = dest // 2
        head = [acc[j * highs + top : j * highs + top + 1, half] for j in range(4 * PARAMS)]
        total = [head[j] + head[2 * PARAMS + j] for j in range(2 * PARAMS)]
        part[dgx % 2, (dgx // 2) * gy_size + dgy] = jnp.concatenate(total, axis=0)

    pl.semaphore_wait(barrier, devices - 1)

    swap = pltpu.make_async_remote_copy(
        src_ref=part.at[1 - core],
        dst_ref=pair_in,
        send_sem=pair_sems.at[0],
        recv_sem=pair_sems.at[1],
        device_id=(gx + 1 - 2 * core, gy),
        device_id_type=MESH,
    )
    swap.start()
    swap.wait()
    chip_sum[...] = part[core] + pair_in[...]

    def chip_copy(i):
        peer = lax.rem(chip + i, chips)
        return pltpu.make_async_remote_copy(
            src_ref=chip_sum.at[peer],
            dst_ref=recv.at[i],
            send_sem=chip_send.at[i],
            recv_sem=chip_recv.at[i],
            device_id=((peer // gy_size) * 2 + core, lax.rem(peer, gy_size)),
            device_id_type=MESH,
        )

    def chip_start(i, carry):
        chip_copy(i).start()
        return carry

    def chip_wait(i, total):
        chip_copy(i).wait()
        return total + recv[i]

    lax.fori_loop(1, chips, chip_start, 0)
    total = lax.fori_loop(1, chips, chip_wait, chip_sum[chip])
    red_ref[...] = total[PARAMS:]
    grad = total[:PARAMS]
    tot_send[0:1, :] = scal_ref[0:1, :]
    tot_send[1:2, :] = scal_ref[1:2, :] + jnp.sum(grad * grad, axis=0, keepdims=True)
    tot_recv[me] = tot_send[...]

    def tot_copy(i):
        peer = lax.rem(me + i, devices)
        return pltpu.make_async_remote_copy(
            src_ref=tot_send,
            dst_ref=tot_recv.at[me],
            send_sem=tot_ssem.at[i],
            recv_sem=tot_rsem.at[i],
            device_id=(peer // gy_size, lax.rem(peer, gy_size)),
            device_id_type=MESH,
        )

    def tot_start(i, carry):
        tot_copy(i).start()
        return carry

    def tot_wait(i, carry):
        tot_copy(i).wait()
        return carry

    lax.fori_loop(1, devices, tot_start, 0)
    lax.fori_loop(1, devices, tot_wait, 0)
    sums = tot_recv[0]
    for d in range(1, devices):
        sums = sums + tot_recv[d]
    sums = jnp.sum(sums, axis=1, keepdims=True)
    cost_ref[...] = sums[0:1] * cost_scale
    norm_ref[...] = jnp.sqrt(sums[1:2] * norm_scale + 1e-06)


def interleaved(array):
    lead = array.shape[:-2]
    n_obs = array.shape[-1]
    blocks = array.reshape(*lead, 2, n_obs // LANES, LANES)
    return jnp.swapaxes(blocks, -3, -2).reshape(*lead, 2 * n_obs // LANES, LANES)


def on_device(
    gx_size, gy_size,
    residual, cam_jacobian, point_jacobian, obs_camera, obs_slot, tile_offset, damping, camera_slot
):
    devices = gx_size * gy_size
    n_obs = residual.shape[1]
    rows = n_obs // LANES
    blocks = damping.shape[0] // LANES
    camera_count = camera_slot.shape[0]
    assert camera_count == devices * LANES and gx_size % 2 == 0
    chips = devices // 2
    highs = camera_count // LOW
    res = interleaved(residual)
    cam_jac = interleaved(jnp.swapaxes(cam_jacobian, 0, 1))
    point_jac = interleaved(jnp.swapaxes(point_jacobian, 0, 1))
    vmem = pl.BlockSpec(memory_space=pltpu.VMEM)
    smem = pl.BlockSpec(memory_space=pltpu.SMEM)
    moved, position, scalars = pl.pallas_call(
        point_kernel,
        out_shape=(
            jax.ShapeDtypeStruct((2, rows, LANES), F32),
            jax.ShapeDtypeStruct((rows, LANES), jnp.int32),
            jax.ShapeDtypeStruct((2, LANES), F32),
        ),
        in_specs=[smem] + [vmem] * 6,
        out_specs=(vmem, vmem, vmem),
        scratch_shapes=[
            pltpu.VMEM((rows * FEATURES, LANES), F32),
            pltpu.VMEM((blocks + 1, FEATURES, LANES), F32),
            pltpu.VMEM((3, blocks + 1, LANES), F32),
        ],
        name="point_part",
    )(
        tile_offset,
        res,
        point_jac,
        obs_camera.reshape(rows, LANES),
        obs_slot.reshape(rows, LANES),
        damping.reshape(blocks, LANES),
        camera_slot.reshape(camera_count // LANES, LANES),
    )
    depth = GROUP * LANES
    dma = pltpu.SemaphoreType.DMA
    reduced, cost, norm = pl.pallas_call(
        functools.partial(
            camera_kernel,
            gx_size,
            gy_size,
            1.0 / (2.0 * n_obs * devices),
            1.0 / (9.0 * camera_count + 3.0 * damping.shape[0] * devices),
        ),
        out_shape=(
            jax.ShapeDtypeStruct((PARAMS, LANES), F32),
            jax.ShapeDtypeStruct((1, 1), F32),
            jax.ShapeDtypeStruct((1, 1), F32),
        ),
        in_specs=[vmem] * 5,
        out_specs=(vmem, vmem, vmem),
        scratch_shapes=[
            pltpu.VMEM((4 * PARAMS * highs, LOW), F32),
            pltpu.VMEM((2, 4 * PARAMS * highs, depth), BF16),
            pltpu.VMEM((2, LOW, depth), BF16),
            pltpu.VMEM((2, 4 * PARAMS, GROUP, LANES), F32),
            pltpu.VMEM((2, chips, 2 * PARAMS, LANES), F32),
            pltpu.VMEM((chips, 2 * PARAMS, LANES), F32),
            pltpu.VMEM((chips, 2 * PARAMS, LANES), F32),
            pltpu.VMEM((chips, 2 * PARAMS, LANES), F32),
            pltpu.VMEM((2, LANES), F32),
            pltpu.VMEM((devices, 2, LANES), F32),
            dma((2,)),
            dma((chips,)),
            dma((chips,)),
            dma((devices,)),
            dma((devices,)),
        ],
        compiler_params=pltpu.CompilerParams(collective_id=0, has_side_effects=True),
        name="camera_part",
    )(cam_jac, res, moved, position, scalars)
    return (reduced, cost.reshape(()), norm.reshape(()))


def solution(mesh):
    return jax.shard_map(
        functools.partial(on_device, mesh.shape["gx"], mesh.shape["gy"]),
        mesh=mesh,
        in_specs=(
            P(None, AXES),
            P(None, None, AXES),
            P(None, None, AXES),
            P(AXES),
            P(AXES),
            P(AXES),
            P(AXES),
            P(),
        ),
        out_specs=(P(None, AXES), P(), P()),
        check_vma=False,
    )
```

time: 476 us -> 40.4 us (0.08)
  matrix products: 174 us -> 0 us
  waiting for transfers between devices: 137 us -> 0 us
  local copies, waits for them, and re-layouts: 95.6 us -> 1.3 us
  blocking collectives: 37.1 us -> 0 us
  Pallas kernels: 0 us -> 34.7 us
  between operations: 19.2 us -> 4.15 us
  other arithmetic: 10.7 us -> 0 us
    dot_general x48 -> x0, matrix products: 174 us -> none  [the longest x32 132 us: add_block(): jnp.dot(block_values, onehot, precision=lax.Precision.HIGHEST)]
    reduce_scatter x1 -> x0, waiting for transfers between devices: 137 us -> none  [on_device(): lax.psum_scatter(both_buffer, ('gx', 'gy'), scatter_dimension=1, tiled=True)]
    gather x1 -> x0, local copies, waits for them, and re-layouts: 90.5 us -> none  [on_device(): cam_slots = camera_slot[obs_camera]]
    psum x1 -> x0, blocking collectives: 37.1 us -> none  [on_device(): cost_total, point_total = lax.psum((cost_part, point_square), ('gx', 'gy'))]
    pallas_call x0 -> x2, Pallas kernels: none -> 34.7 us  [the longest x1 28 us: on_device(): pl.pallas_call(functools.partial(camera_kernel, gx_size, gy_size, 1.0 / (...]
    reduce_sum x7 -> x0, other arithmetic: 10.2 us -> none  [the longest x1 2.98 us: on_device(): grad_obs = jnp.sum(cam_jacobian * residual[:, None, :], axis=0)]
  transfers between devices with their start and end apart: 1 -> 0, of which waited for: 1 -> 0; matrix products, arithmetic and copies ran while one was open for 0% -> 0% of each run, Pallas kernels for 0% -> 0%
where the time goes in v1:
time: 40.4 us; the launch traced here: 40.2 us
  Pallas kernels  34.7 us (86%)
  between operations  4.15 us (10%)
  local copies, waits for them, and re-layouts  1.3 us (3%)
    pallas_call x1, Pallas kernels, on_device(): pl.pallas_call(functools.partial(camera_kernel, gx_size, gy_size, 1.0 / (...  28 us
    pallas_call x1, Pallas kernels, on_device(): pl.pallas_call(point_kernel, out_shape=(jax.ShapeDtypeStruct((2, rows, LA...  6.77 us
    unnamed x1, local copies, waits for them, and re-layouts  1.3 us

profile of v1, /device:TPU:0, one launch (start us, length us, event | category | flops | bytes accessed | tf_op | source)
XLA Modules:
  0.0 40.2 jit_solution(531122524881097491)
XLA Ops:
  0.6 6.8 %point_part.1 = (f32[2,128,128]{2,1,0:T(8,128)}, s32[128,128]{1,0:T(8,128)}, f32[2,128]{1,0:T(2,128)}) custom-call(s32[32]{0:T(128)} %toff_ref.1, f32[256,128]{1,0:T(8,128)} %bitcast.26, f32[3,256,128]{2,1,0:T(8,128)} %bitcast.28, s32[128,128]{1,0:T(8,128)} %bitcast.29, s32[128,128]{1,0:T(8,128)} %bitcast.30, f32[16,128]{1,0:T(8,128)} %bitcast.32, ...), custom_call_target="tpu_custom_call" | custom-call | tf_op jit(solution)/shard_map/point_part/pallas_call | solution.py:339
  7.4 28.0 %camera_part.1 = (f32[9,128]{1,0:T(8,128)}, f32[1,1]{1,0:T(1,128)}, f32[1,1]{1,0:T(1,128)}) custom-call(f32[9,256,128]{2,1,0:T(8,128)} %bitcast.25, f32[256,128]{1,0:T(8,128)} %bitcast.27, f32[2,128,128]{2,1,0:T(8,128)} %get-tuple-element.9.w_ref, s32[128,128]{1,0:T(8,128)} %get-tuple-element.10.pos_ref, f32[2,128]{1,0:T(2,128)} %get-tuple-element.11.scal_ref), custom_call_target="tpu_custom_call" | custom-call | tf_op jit(solution)/shard_map/camera_part/pallas_call | solution.py:365
  35.4 1.3 %copy.17 = f32[9,128]{1,0:T(8,128)} copy(f32[9,128]{1,0:T(8,128)} %get-tuple-element.18) | data formatting | bytes 9216

commit v2 on v1

--- a/solution.py
+++ b/solution.py
@@ -55,9 +55,15 @@
 
 
 def point_kernel(
-    toff_ref, res_ref, pj_ref, cam_ref, slot_ref, damp_ref, cslot_ref,
-    w_ref, pos_ref, scal_ref, feat, sums, steps,
+    toff_ref, res_hbm, pj_hbm, cam_ref, slot_ref, damp_ref, cslot_ref,
+    w_ref, pos_ref, scal_ref, feat, sums, steps, res_ref, pj_ref, in_sems,
 ):
+    copies = [
+        pltpu.make_async_copy(res_hbm, res_ref, in_sems.at[0]),
+        pltpu.make_async_copy(pj_hbm, pj_ref, in_sems.at[1]),
+    ]
+    for copy in copies:
+        copy.start()
     rows = cam_ref.shape[0]
     tiles = toff_ref.shape[0]
     tile_rows = rows // tiles
@@ -75,7 +81,7 @@
             for part in range(2)
         ]
 
-    def group_step(group, cost):
+    def position_step(group, carry):
         at = pl.ds(pl.multiple_of(group * GROUP, GROUP), GROUP)
         camera = cam_ref[at, :]
         high = camera >> 7
@@ -84,6 +90,13 @@
         for t in range(table_rows):
             position = jnp.where(high == t, lane_take(cslot_ref[t : t + 1, :], low), position)
         pos_ref[at, :] = position
+        return carry
+
+    lax.fori_loop(0, groups, position_step, 0, unroll=4)
+    for copy in copies:
+        copy.wait()
+
+    def group_step(group, cost):
         res = pair(res_ref, group)
         jac = [pair(pj_ref, group, (k,)) for k in range(3)]
         values = [jac[k][0] * res[0] + jac[k][1] * res[1] for k in range(3)]
@@ -175,10 +188,10 @@
 
 def camera_kernel(
     gx_size, gy_size, cost_scale, norm_scale,
-    cj_ref, res_ref, w_ref, pos_ref, scal_ref,
+    cj_hbm, res_ref, w_ref, pos_ref, scal_ref,
     red_ref, cost_ref, norm_ref,
-    acc, left, right, rowbuf, part, pair_in, chip_sum, recv, tot_send, tot_recv,
-    pair_sems, chip_send, chip_recv, tot_ssem, tot_rsem,
+    cj_ref, acc, left, right, rowbuf, part, pair_in, chip_sum, recv, tot_send, tot_recv,
+    in_sems, pair_sems, chip_send, chip_recv, tot_ssem, tot_rsem,
 ):
     devices = gx_size * gy_size
     chips = devices // 2
@@ -187,6 +200,19 @@
     me = gx * gy_size + gy
     core = lax.rem(gx, 2)
     chip = (gx // 2) * gy_size + gy
+    rows = pos_ref.shape[0]
+    steps = rows // (2 * GROUP)
+    highs = devices * LANES // LOW
+
+    def cj_copy(step):
+        at = pl.ds(pl.multiple_of(step * (4 * GROUP), 4 * GROUP), 4 * GROUP)
+        return pltpu.make_async_copy(cj_hbm.at[:, at, :], cj_ref.at[:, at, :], in_sems.at[step])
+
+    def cj_start(step, carry):
+        cj_copy(step).start()
+        return carry
+
+    lax.fori_loop(0, steps, cj_start, 0)
 
     barrier = pltpu.get_barrier_semaphore()
 
@@ -199,89 +225,94 @@
 
     lax.fori_loop(1, devices, greet, 0)
 
-    rows = pos_ref.shape[0]
-    highs = devices * LANES // LOW
     lows = lax.broadcasted_iota(jnp.int32, (LOW, LANES), 0)
     tops = lax.broadcasted_iota(jnp.int32, (highs, LANES), 0)
     acc[...] = jnp.zeros_like(acc)
 
-    def build(group, buf):
+    def add_group(which, group, buf):
         at = pl.ds(pl.multiple_of(group * GROUP, GROUP), GROUP)
         even = pl.ds(group * (2 * GROUP), GROUP, stride=2)
         odd = pl.ds(group * (2 * GROUP) + 1, GROUP, stride=2)
-        res0, res1 = res_ref[even, :], res_ref[odd, :]
-        w0, w1 = w_ref[0, at, :], w_ref[1, at, :]
+        if which == 0:
+            factor0, factor1 = res_ref[even, :], res_ref[odd, :]
+        else:
+            factor0, factor1 = w_ref[0, at, :], w_ref[1, at, :]
         for m in range(PARAMS):
-            jac0, jac1 = cj_ref[m, even, :], cj_ref[m, odd, :]
-            for j, value in ((m, jac0 * res0 + jac1 * res1), (m + PARAMS, jac0 * w0 + jac1 * w1)):
-                head = value.astype(BF16).astype(F32)
-                rowbuf[buf, j] = head
-                rowbuf[buf, 2 * PARAMS + j] = value - head
+            value = cj_ref[m, even, :] * factor0 + cj_ref[m, odd, :] * factor1
+            head = value.astype(BF16).astype(F32)
+            rowbuf[buf, m] = head
+            rowbuf[buf, PARAMS + m] = value - head
         for r in range(GROUP):
             position = pos_ref[pl.ds(group * GROUP + r, 1), :]
             cols = slice(r * LANES, (r + 1) * LANES)
-            right[buf, :, cols] = jnp.where(lows == (position & (LOW - 1)), 1.0, 0.0).astype(BF16)
+            if which == 0:
+                onehot = jnp.where(lows == (position & (LOW - 1)), 1.0, 0.0).astype(BF16)
+                right[group, :, cols] = onehot
             top = jnp.where(tops == (position >> LOW_BITS), 1.0, 0.0).astype(BF16)
-            for j in range(4 * PARAMS):
+            for j in range(2 * PARAMS):
                 row = jnp.broadcast_to(rowbuf[buf, j, r : r + 1, :], (highs, LANES)).astype(BF16)
                 left[buf, j * highs : (j + 1) * highs, cols] = row * top
-
-    def two_groups(step, carry):
+        acc[which] += nt_dot(left[buf], right[group])
+
+    def grad_groups(step, carry):
+        cj_copy(step).wait()
         for buf in range(2):
-            build(step * 2 + buf, buf)
-            acc[...] += nt_dot(left[buf], right[buf])
-        return carry
-
-    lax.fori_loop(0, rows // (2 * GROUP), two_groups, 0)
-
-    for dest in range(devices):
-        dgx, dgy = dest // gy_size, dest % gy_size
-        half = slice((dest % 2) * LANES, (dest % 2 + 1) * LANES)
-        top = dest // 2
-        head = [acc[j * highs + top : j * highs + top + 1, half] for j in range(4 * PARAMS)]
-        total = [head[j] + head[2 * PARAMS + j] for j in range(2 * PARAMS)]
-        part[dgx % 2, (dgx // 2) * gy_size + dgy] = jnp.concatenate(total, axis=0)
-
-    pl.semaphore_wait(barrier, devices - 1)
-
-    swap = pltpu.make_async_remote_copy(
-        src_ref=part.at[1 - core],
-        dst_ref=pair_in,
-        send_sem=pair_sems.at[0],
-        recv_sem=pair_sems.at[1],
-        device_id=(gx + 1 - 2 * core, gy),
-        device_id_type=MESH,
-    )
-    swap.start()
-    swap.wait()
-    chip_sum[...] = part[core] + pair_in[...]
-
-    def chip_copy(i):
+            add_group(0, step * 2 + buf, buf)
+        return carry
+
+    def red_groups(step, carry):
+        for buf in range(2):
+            add_group(1, step * 2 + buf, buf)
+        return carry
+
+    def pack(which):
+        for dest in range(devices):
+            dgx, dgy = dest // gy_size, dest % gy_size
+            half = slice((dest % 2) * LANES, (dest % 2 + 1) * LANES)
+            for m in range(PARAMS):
+                head = m * highs + dest // 2
+                rest = (PARAMS + m) * highs + dest // 2
+                part[which, dgx % 2, (dgx // 2) * gy_size + dgy, :, m * LANES : (m + 1) * LANES] = (
+                    acc[which, head : head + 1, half] + acc[which, rest : rest + 1, half]
+                )
+
+    def swap(which):
+        return pltpu.make_async_remote_copy(
+            src_ref=part.at[which, 1 - core],
+            dst_ref=pair_in.at[which],
+            send_sem=pair_sems.at[which, 0],
+            recv_sem=pair_sems.at[which, 1],
+            device_id=(gx + 1 - 2 * core, gy),
+            device_id_type=MESH,
+        )
+
+    def chip_copy(which, i):
         peer = lax.rem(chip + i, chips)
         return pltpu.make_async_remote_copy(
-            src_ref=chip_sum.at[peer],
-            dst_ref=recv.at[i],
-            send_sem=chip_send.at[i],
-            recv_sem=chip_recv.at[i],
+            src_ref=chip_sum.at[which, peer],
+            dst_ref=recv.at[which, i],
+            send_sem=chip_send.at[which, i],
+            recv_sem=chip_recv.at[which, i],
             device_id=((peer // gy_size) * 2 + core, lax.rem(peer, gy_size)),
             device_id_type=MESH,
         )
 
-    def chip_start(i, carry):
-        chip_copy(i).start()
-        return carry
-
-    def chip_wait(i, total):
-        chip_copy(i).wait()
-        return total + recv[i]
-
-    lax.fori_loop(1, chips, chip_start, 0)
-    total = lax.fori_loop(1, chips, chip_wait, chip_sum[chip])
-    red_ref[...] = total[PARAMS:]
-    grad = total[:PARAMS]
-    tot_send[0:1, :] = scal_ref[0:1, :]
-    tot_send[1:2, :] = scal_ref[1:2, :] + jnp.sum(grad * grad, axis=0, keepdims=True)
-    tot_recv[me] = tot_send[...]
+    def spread(which):
+        swap(which).wait()
+        chip_sum[which] = part[which, core] + pair_in[which]
+
+        def chip_start(i, carry):
+            chip_copy(which, i).start()
+            return carry
+
+        lax.fori_loop(1, chips, chip_start, 0)
+
+    def gather(which):
+        def chip_wait(i, total):
+            chip_copy(which, i).wait()
+            return total + recv[which, i]
+
+        return lax.fori_loop(1, chips, chip_wait, chip_sum[which, chip])
 
     def tot_copy(i):
         peer = lax.rem(me + i, devices)
@@ -302,7 +333,32 @@
         tot_copy(i).wait()
         return carry
 
+    early = steps // 4
+    lax.fori_loop(0, steps, grad_groups, 0)
+    pack(0)
+    pl.semaphore_wait(barrier, devices - 1)
+    swap(0).start()
+    lax.fori_loop(0, early, red_groups, 0)
+    spread(0)
+    lax.fori_loop(early, steps, red_groups, 0)
+    pack(1)
+    swap(1).start()
+
+    grad = gather(0)
+    square = jnp.zeros((1, LANES), F32)
+    for m in range(PARAMS):
+        column = grad[:, m * LANES : (m + 1) * LANES]
+        square = square + column * column
+    tot_send[0:1, :] = scal_ref[0:1, :]
+    tot_send[1:2, :] = scal_ref[1:2, :] + square
+    tot_recv[me] = tot_send[...]
     lax.fori_loop(1, devices, tot_start, 0)
+
+    spread(1)
+    reduced = gather(1)
+    for m in range(PARAMS):
+        red_ref[m : m + 1, :] = reduced[:, m * LANES : (m + 1) * LANES]
+
     lax.fori_loop(1, devices, tot_wait, 0)
     sums = tot_recv[0]
     for d in range(1, devices):
@@ -335,6 +391,7 @@
     cam_jac = interleaved(jnp.swapaxes(cam_jacobian, 0, 1))
     point_jac = interleaved(jnp.swapaxes(point_jacobian, 0, 1))
     vmem = pl.BlockSpec(memory_space=pltpu.VMEM)
+    hbm = pl.BlockSpec(memory_space=pl.ANY)
     smem = pl.BlockSpec(memory_space=pltpu.SMEM)
     moved, position, scalars = pl.pallas_call(
         point_kernel,
@@ -343,12 +400,15 @@
             jax.ShapeDtypeStruct((rows, LANES), jnp.int32),
             jax.ShapeDtypeStruct((2, LANES), F32),
         ),
-        in_specs=[smem] + [vmem] * 6,
+        in_specs=[smem, hbm, hbm] + [vmem] * 4,
         out_specs=(vmem, vmem, vmem),
         scratch_shapes=[
             pltpu.VMEM((rows * FEATURES, LANES), F32),
             pltpu.VMEM((blocks + 1, FEATURES, LANES), F32),
             pltpu.VMEM((3, blocks + 1, LANES), F32),
+            pltpu.VMEM(res.shape, F32),
+            pltpu.VMEM(point_jac.shape, F32),
+            pltpu.SemaphoreType.DMA((2,)),
         ],
         name="point_part",
     )(
@@ -375,22 +435,24 @@
             jax.ShapeDtypeStruct((1, 1), F32),
             jax.ShapeDtypeStruct((1, 1), F32),
         ),
-        in_specs=[vmem] * 5,
+        in_specs=[hbm] + [vmem] * 4,
         out_specs=(vmem, vmem, vmem),
         scratch_shapes=[
-            pltpu.VMEM((4 * PARAMS * highs, LOW), F32),
-            pltpu.VMEM((2, 4 * PARAMS * highs, depth), BF16),
-            pltpu.VMEM((2, LOW, depth), BF16),
-            pltpu.VMEM((2, 4 * PARAMS, GROUP, LANES), F32),
-            pltpu.VMEM((2, chips, 2 * PARAMS, LANES), F32),
-            pltpu.VMEM((chips, 2 * PARAMS, LANES), F32),
-            pltpu.VMEM((chips, 2 * PARAMS, LANES), F32),
-            pltpu.VMEM((chips, 2 * PARAMS, LANES), F32),
+            pltpu.VMEM(cam_jac.shape, F32),
+            pltpu.VMEM((2, 2 * PARAMS * highs, LOW), F32),
+            pltpu.VMEM((2, 2 * PARAMS * highs, depth), BF16),
+            pltpu.VMEM((rows // GROUP, LOW, depth), BF16),
+            pltpu.VMEM((2, 2 * PARAMS, GROUP, LANES), F32),
+            pltpu.VMEM((2, 2, chips, 1, PARAMS * LANES), F32),
+            pltpu.VMEM((2, chips, 1, PARAMS * LANES), F32),
+            pltpu.VMEM((2, chips, 1, PARAMS * LANES), F32),
+            pltpu.VMEM((2, chips, 1, PARAMS * LANES), F32),
             pltpu.VMEM((2, LANES), F32),
             pltpu.VMEM((devices, 2, LANES), F32),
-            dma((2,)),
-            dma((chips,)),
-            dma((chips,)),
+            dma((rows // (2 * GROUP),)),
+            dma((2, 2)),
+            dma((2, chips)),
+            dma((2, chips)),
             dma((devices,)),
             dma((devices,)),
         ],

time: 40.4 us -> 37.8 us (0.936)
  Pallas kernels: 34.7 us -> 32.1 us
    pallas_call x1, Pallas kernels: 28 us -> 25.5 us  [on_device(): pl.pallas_call(functools.partial(camera_kernel, gx_size, gy_size, 1.0 / (...]
where the time goes in v2:
time: 37.8 us; the launch traced here: 37.5 us
  Pallas kernels  32.1 us (85%)
  between operations  4.16 us (11%)
  local copies, waits for them, and re-layouts  1.3 us (3%)
    pallas_call x1, Pallas kernels, on_device(): pl.pallas_call(functools.partial(camera_kernel, gx_size, gy_size, 1.0 / (...  25.5 us
    pallas_call x1, Pallas kernels, on_device(): pl.pallas_call(point_kernel, out_shape=(jax.ShapeDtypeStruct((2, rows, LA...  6.57 us
    unnamed x1, local copies, waits for them, and re-layouts  1.3 us

profile of v2, /device:TPU:0, one launch (start us, length us, event | category | flops | bytes accessed | tf_op | source)
XLA Modules:
  0.0 37.5 jit_solution(1635403019333004648)
XLA Ops:
  0.6 6.6 %point_part.1 = (f32[2,128,128]{2,1,0:T(8,128)}, s32[128,128]{1,0:T(8,128)}, f32[2,128]{1,0:T(2,128)}) custom-call(s32[32]{0:T(128)} %toff_ref.1, f32[256,128]{1,0:T(8,128)} %bitcast.26, f32[3,256,128]{2,1,0:T(8,128)} %bitcast.28, s32[128,128]{1,0:T(8,128)} %bitcast.29, s32[128,128]{1,0:T(8,128)} %bitcast.30, f32[16,128]{1,0:T(8,128)} %bitcast.32, ...), custom_call_target="tpu_custom_call" | custom-call | tf_op jit(solution)/shard_map/point_part/pallas_call | solution.py:396
  7.2 25.5 %camera_part.1 = (f32[9,128]{1,0:T(8,128)}, f32[1,1]{1,0:T(1,128)}, f32[1,1]{1,0:T(1,128)}) custom-call(f32[9,256,128]{2,1,0:T(8,128)} %bitcast.25, f32[256,128]{1,0:T(8,128)} %bitcast.27, f32[2,128,128]{2,1,0:T(8,128)} %get-tuple-element.9.w_ref, s32[128,128]{1,0:T(8,128)} %get-tuple-element.10.pos_ref, f32[2,128]{1,0:T(2,128)} %get-tuple-element.11.scal_ref), custom_call_target="tpu_custom_call" | custom-call | tf_op jit(solution)/shard_map/camera_part/pallas_call | solution.py:425
  32.7 1.3 %copy.17 = f32[9,128]{1,0:T(8,128)} copy(f32[9,128]{1,0:T(8,128)} %get-tuple-element.18) | data formatting | bytes 9216

commit v3 on v2

--- a/solution.py
+++ b/solution.py
@@ -13,6 +13,7 @@
 BF16 = jnp.bfloat16
 LANES = 128
 GROUP = 8
+SLOTS = 2
 LOW_BITS = 8
 LOW = 1 << LOW_BITS
 PARAMS = 9
@@ -89,7 +90,8 @@
         position = jnp.zeros_like(camera)
         for t in range(table_rows):
             position = jnp.where(high == t, lane_take(cslot_ref[t : t + 1, :], low), position)
-        pos_ref[at, :] = position
+        pos_ref[0, at, :] = (position & (LOW - 1)).astype(F32)
+        pos_ref[1, at, :] = (position >> LOW_BITS).astype(F32)
         return carry
 
     lax.fori_loop(0, groups, position_step, 0, unroll=4)
@@ -200,7 +202,7 @@
     me = gx * gy_size + gy
     core = lax.rem(gx, 2)
     chip = (gx // 2) * gy_size + gy
-    rows = pos_ref.shape[0]
+    rows = pos_ref.shape[1]
     steps = rows // (2 * GROUP)
     highs = devices * LANES // LOW
 
@@ -225,8 +227,10 @@
 
     lax.fori_loop(1, devices, greet, 0)
 
-    lows = lax.broadcasted_iota(jnp.int32, (LOW, LANES), 0)
-    tops = lax.broadcasted_iota(jnp.int32, (highs, LANES), 0)
+    lows = lax.broadcasted_iota(jnp.int32, (LOW, LANES), 0).astype(F32).astype(BF16)
+    tops = lax.broadcasted_iota(jnp.int32, (highs, LANES), 0).astype(F32).astype(BF16)
+    one = jnp.ones((), BF16)
+    none = jnp.zeros((), BF16)
     acc[...] = jnp.zeros_like(acc)
 
     def add_group(which, group, buf):
@@ -243,26 +247,28 @@
             rowbuf[buf, m] = head
             rowbuf[buf, PARAMS + m] = value - head
         for r in range(GROUP):
-            position = pos_ref[pl.ds(group * GROUP + r, 1), :]
+            row_at = pl.ds(group * GROUP + r, 1)
             cols = slice(r * LANES, (r + 1) * LANES)
             if which == 0:
-                onehot = jnp.where(lows == (position & (LOW - 1)), 1.0, 0.0).astype(BF16)
-                right[group, :, cols] = onehot
-            top = jnp.where(tops == (position >> LOW_BITS), 1.0, 0.0).astype(BF16)
+                low = jnp.broadcast_to(pos_ref[0, row_at, :], (LOW, LANES)).astype(BF16)
+                right[group, :, cols] = jnp.where(lows == low, one, none)
+            high = jnp.broadcast_to(pos_ref[1, row_at, :], (highs, LANES)).astype(BF16)
+            top = jnp.where(tops == high, one, none)
             for j in range(2 * PARAMS):
                 row = jnp.broadcast_to(rowbuf[buf, j, r : r + 1, :], (highs, LANES)).astype(BF16)
                 left[buf, j * highs : (j + 1) * highs, cols] = row * top
         acc[which] += nt_dot(left[buf], right[group])
 
     def grad_groups(step, carry):
-        cj_copy(step).wait()
-        for buf in range(2):
-            add_group(0, step * 2 + buf, buf)
+        for buf in range(SLOTS):
+            if buf % 2 == 0:
+                cj_copy(step * (SLOTS // 2) + buf // 2).wait()
+            add_group(0, step * SLOTS + buf, buf)
         return carry
 
     def red_groups(step, carry):
-        for buf in range(2):
-            add_group(1, step * 2 + buf, buf)
+        for buf in range(SLOTS):
+            add_group(1, step * SLOTS + buf, buf)
         return carry
 
     def pack(which):
@@ -333,14 +339,15 @@
         tot_copy(i).wait()
         return carry
 
-    early = steps // 4
-    lax.fori_loop(0, steps, grad_groups, 0)
+    loops = rows // (SLOTS * GROUP)
+    early = loops // 4
+    lax.fori_loop(0, loops, grad_groups, 0)
     pack(0)
     pl.semaphore_wait(barrier, devices - 1)
     swap(0).start()
     lax.fori_loop(0, early, red_groups, 0)
     spread(0)
-    lax.fori_loop(early, steps, red_groups, 0)
+    lax.fori_loop(early, loops, red_groups, 0)
     pack(1)
     swap(1).start()
 
@@ -397,7 +404,7 @@
         point_kernel,
         out_shape=(
             jax.ShapeDtypeStruct((2, rows, LANES), F32),
-            jax.ShapeDtypeStruct((rows, LANES), jnp.int32),
+            jax.ShapeDtypeStruct((2, rows, LANES), F32),
             jax.ShapeDtypeStruct((2, LANES), F32),
         ),
         in_specs=[smem, hbm, hbm] + [vmem] * 4,
@@ -440,9 +447,9 @@
         scratch_shapes=[
             pltpu.VMEM(cam_jac.shape, F32),
             pltpu.VMEM((2, 2 * PARAMS * highs, LOW), F32),
-            pltpu.VMEM((2, 2 * PARAMS * highs, depth), BF16),
+            pltpu.VMEM((SLOTS, 2 * PARAMS * highs, depth), BF16),
             pltpu.VMEM((rows // GROUP, LOW, depth), BF16),
-            pltpu.VMEM((2, 2 * PARAMS, GROUP, LANES), F32),
+            pltpu.VMEM((SLOTS, 2 * PARAMS, GROUP, LANES), F32),
             pltpu.VMEM((2, 2, chips, 1, PARAMS * LANES), F32),
             pltpu.VMEM((2, chips, 1, PARAMS * LANES), F32),
             pltpu.VMEM((2, chips, 1, PARAMS * LANES), F32),

time: 37.8 us -> 37.3 us (0.987)
  Pallas kernels: 32.1 us -> 31.4 us
    pallas_call x1, Pallas kernels: 25.5 us -> 24.9 us  [on_device(): pl.pallas_call(functools.partial(camera_kernel, gx_size, gy_size, 1.0 / (...]
where the time goes in v3:
time: 37.3 us; the launch traced here: 37 us
  Pallas kernels  31.4 us (84%)
  between operations  4.28 us (11%)
  local copies, waits for them, and re-layouts  1.3 us (3%)
    pallas_call x1, Pallas kernels, on_device(): pl.pallas_call(functools.partial(camera_kernel, gx_size, gy_size, 1.0 / (...  24.9 us
    pallas_call x1, Pallas kernels, on_device(): pl.pallas_call(point_kernel, out_shape=(jax.ShapeDtypeStruct((2, rows, LA...  6.57 us
    unnamed x1, local copies, waits for them, and re-layouts  1.3 us

profile of v3, /device:TPU:0, one launch (start us, length us, event | category | flops | bytes accessed | tf_op | source)
XLA Modules:
  0.0 37.0 jit_solution(2426831761440299533)
XLA Ops:
  0.6 6.6 %point_part.1 = (f32[2,128,128]{2,1,0:T(8,128)}, f32[2,128,128]{2,1,0:T(8,128)}, f32[2,128]{1,0:T(2,128)}) custom-call(s32[32]{0:T(128)} %toff_ref.1, f32[256,128]{1,0:T(8,128)} %bitcast.26, f32[3,256,128]{2,1,0:T(8,128)} %bitcast.28, s32[128,128]{1,0:T(8,128)} %bitcast.29, s32[128,128]{1,0:T(8,128)} %bitcast.30, f32[16,128]{1,0:T(8,128)} %bitcast.32, ...), custom_call_target="tpu_custom_call" | custom-call | tf_op jit(solution)/shard_map/point_part/pallas_call | solution.py:403
  7.2 24.9 %camera_part.1 = (f32[9,128]{1,0:T(8,128)}, f32[1,1]{1,0:T(1,128)}, f32[1,1]{1,0:T(1,128)}) custom-call(f32[9,256,128]{2,1,0:T(8,128)} %bitcast.25, f32[256,128]{1,0:T(8,128)} %bitcast.27, f32[2,128,128]{2,1,0:T(8,128)} %get-tuple-element.9.w_ref, f32[2,128,128]{2,1,0:T(8,128)} %get-tuple-element.10.pos_ref, f32[2,128]{1,0:T(2,128)} %get-tuple-element.11.scal_ref), custom_call_target="tpu_custom_call" | custom-call | tf_op jit(solution)/shard_map/camera_part/pallas_call | solution.py:432
  32.1 1.3 %copy.17 = f32[9,128]{1,0:T(8,128)} copy(f32[9,128]{1,0:T(8,128)} %get-tuple-element.18) | data formatting | bytes 9216
